TPU v7x, 32 devices: a whole 2x2x4 slice. The times are simulated.
32 devices in a mesh: row: 8 (over z, y), col: 4 (over x, core).
Axes of the slice: x: 2, y: 2, z: 4, core: 2. Of those that a mesh axis runs over, the one named last changes fastest.
Arguments:
- amplitudes: float32 [128, 512, 512], P(('row', 'col')), may hold values from -6 to 6
- integrals: float32 [512, 1024, 1024], P(('row', 'col')), may hold values from -0.01171875 to 0.01171875
- coupling: float32 [512, 32, 1024], P(('row', 'col')), may hold values from -0.046875 to 0.046875
- task_table: int32 [32, 16, 2], replicated, may hold values from -1 to 15, as said below
Outputs:
- residual: float32 [128, 1024], P(('row', 'col'))
Inputs may be any that keep to these rules, and one draw needn't show every extreme that they name: `task_table`: every virtual tile pair (C, D), C and D in 0 to 15, appears in exactly one slot. In each device's row the valid slots come first and the rest hold -1 in both entries. Some device has all 16 slots valid and some device has none. `integrals`: slots that task_table marks -1 are not read.
All inputs are finite; a program needn't handle non-finite values.
Results may differ from a plain program's by a relative error of at most 0.0003.
Values sent between devices are 32-bit elements; how exact they have to be, the bound alone decides.
A program may use at most 192 MiB of HBM per device.

v0:
```python
import jax
import jax.numpy as jnp
from jax import lax
from jax.sharding import PartitionSpec as P

TB = 32
NVT = 16


def tile_stack(amplitudes):
    local_rows = amplitudes.shape[0]
    shaped = amplitudes.reshape(local_rows, NVT, TB, NVT, TB)
    return jnp.transpose(shaped, (1, 3, 0, 2, 4)).reshape(NVT * NVT, local_rows, TB * TB)


def body(amplitudes, integrals, coupling, task_table):
    row_count = lax.axis_size("row")
    col_count = lax.axis_size("col")
    devices_all = row_count * col_count
    local_rows = amplitudes.shape[0]
    slot_total = integrals.shape[0]
    total_rows = devices_all * local_rows
    stacked = tile_stack(amplitudes)
    pair_ids = jnp.maximum(task_table[:, :, 0] * NVT + task_table[:, :, 1], 0).reshape(-1)
    outgoing = jnp.take(stacked, pair_ids, axis=0).reshape(
        devices_all, slot_total, local_rows, TB * TB
    )
    arrived = lax.all_to_all(outgoing, ("row", "col"), split_axis=0, concat_axis=0, tiled=True)
    own_index = lax.axis_index(("row", "col"))
    own_tasks = lax.dynamic_index_in_dim(task_table, own_index, 0, keepdims=False)
    valid_count = jnp.sum((own_tasks[:, 0] >= 0).astype(jnp.int32))

    def add_tile(slot_index, partial_value):
        tile_rows = lax.dynamic_index_in_dim(arrived, slot_index, 1, keepdims=False).reshape(
            total_rows, TB * TB
        )
        integral_tile = lax.dynamic_index_in_dim(integrals, slot_index, 0, keepdims=False)
        product = lax.dot_general(
            tile_rows,
            integral_tile,
            (((1,), (1,)), ((), ())),
            precision=lax.Precision.HIGHEST,
            preferred_element_type=jnp.float32,
        )
        return partial_value + product

    ladder = lax.fori_loop(0, valid_count, add_tile, jnp.zeros((total_rows, TB * TB), jnp.float32))
    first_tile = amplitudes[:, :TB, :]
    pieces = lax.all_to_all(first_tile, ("row", "col"), split_axis=2, concat_axis=0, tiled=True)
    width_part = pieces.shape[2]
    occupied = coupling.shape[1]
    window = total_rows // occupied
    regrouped = jnp.transpose(
        pieces.reshape(window, occupied, TB, width_part), (0, 2, 3, 1)
    ).reshape(window * TB, width_part * occupied)
    coupling_rows = coupling.reshape(width_part * occupied, occupied * TB)
    hole_term = jnp.dot(
        regrouped,
        coupling_rows,
        precision=lax.Precision.HIGHEST,
        preferred_element_type=jnp.float32,
    )
    hole_term = jnp.transpose(hole_term.reshape(window, TB, occupied, TB), (0, 2, 1, 3)).reshape(
        total_rows, TB * TB
    )
    ladder_share = lax.psum_scatter(ladder, ("row", "col"), scatter_dimension=0, tiled=True)
    hole_share = lax.psum_scatter(hole_term, ("row", "col"), scatter_dimension=0, tiled=True)
    return ladder_share + hole_share


def solution(mesh):
    in_specs = (
        P(("row", "col"), None, None),
        P(("row", "col"), None, None),
        P(("row", "col"), None, None),
        P(),
    )
    out_specs = P(("row", "col"), None)
    return jax.shard_map(body, mesh=mesh, in_specs=in_specs, out_specs=out_specs, check_vma=False)
```

profile of v0, /device:TPU:0, one launch (start us, length us, event | category | flops | bytes accessed | tf_op | source)
XLA Modules:
  0.0 560.8 jit_solution(12133687028643890599)
XLA Ops:
  6.5 1.0 slice.15
  7.5 0.4 copy.37
  7.9 1.4 reshape.96
  9.3 7.3 %all-to-all-start.1 = ((f32[32,1,2048]{2,1,0:T(1,128)}), f32[32,1,2048]{2,1,0:T(1,128)S(1)}, u32[]{:S(2)}, u32[]{:S(2)}) async-start(f32[32,1,2048]{2,1,0:T(1,128)} %reshape.96), calls=%async_computation.1 | async-start | bytes 524288 | tf_op jit(solution)/shard_map/all_to_all | solution.py:49
  16.6 0.0 copy-start.1
  16.6 11.1 %reshape.79 = f32[4,16,32,16,32]{4,3,2,1,0:T(8,128)} reshape(f32[4,512,512]{2,1,0:T(8,128)} %param.6) | data formatting | bytes 8388608 | tf_op jit(solution)/shard_map/reshape | solution.py:12
  27.7 0.0 copy-done.1
  27.7 0.1 copy.35
  27.8 0.1 reshape.86
  27.9 15.8 %copy.46 = f32[4,16,32,16,32]{4,2,3,1,0:T(8,128)} copy(f32[4,16,32,16,32]{4,3,2,1,0:T(8,128)} %reshape.79) | data formatting | bytes 8388608 | tf_op jit(solution)/shard_map/reshape | solution.py:12
  43.7 13.7 %reshape.80 = f32[256,4,1024]{2,0,1:T(8,128)} reshape(f32[16,16,4,32,32]{4,3,1,0,2:T(8,128)} %bitcast.49) | data formatting | bytes 8388608 | tf_op jit(solution)/shard_map/reshape | solution.py:13
  57.4 6.8 %copy.36 = f32[256,4,1024]{2,1,0:T(4,128)} copy(f32[256,4,1024]{2,0,1:T(8,128)} %reshape.80) | data formatting | bytes 8388608 | tf_op jit(solution)/shard_map/reshape | solution.py:13
  64.2 0.1 copy.33
  64.3 22.9 %gather_fusion = f32[512,4,1024]{2,1,0:T(4,128)} fusion(f32[256,4,1024]{2,1,0:T(4,128)} %copy.36, s32[1024]{0:T(1024)S(1)} %pad_clamp_fusion), kind=kCustom, calls=%fused_computation | custom fusion | bytes 16779264 | tf_op jit(solution)/shard_map/jit(_take)/gather | solution.py:25
  87.2 7.7 %broadcast_select_fusion = f32[32,16,4,1024]{3,2,1,0:T(4,128)} fusion(f32[32,16,4,1024]{3,2,1,0:T(4,128)} %bitcast.50, pred[32,16]{1,0:T(8,128)(4,1)S(1)} %copy.33), kind=kLoop, calls=%fused_computation.8 | loop fusion | flops 2097152 | bytes 16777728 | tf_op jit(solution)/shard_map/jit(_take)/select_n | solution.py:25
  95.0 0.0 copy-start
  95.0 0.0 all-to-all-done.1
  95.0 6.0 %all-to-all-start = ((f32[32,16,4,1024]{3,2,1,0:T(4,128)}), f32[32,16,4,1024]{3,2,1,0:T(4,128)}, u32[]{:S(2)}, u32[]{:S(2)}) async-start(f32[32,16,4,1024]{3,2,1,0:T(4,128)} %broadcast_select_fusion), calls=%async_computation | async-start | bytes 16777216 | tf_op jit(solution)/shard_map/all_to_all | solution.py:28
  100.9 0.0 all-reduce.3.cloned.1.call-start
  101.0 0.1 constant_dynamic-slice_fusion.2
  101.1 0.1 copy.30
  101.2 0.0 copy-done
  101.2 2.0 copy.41
  103.2 0.6 fusion.8
  103.8 0.5 broadcast.61
  104.4 1.2 reduce.1
  105.6 0.5 reshape.97
  106.2 0.1 copy.38
  106.3 0.1 copy.39
  106.4 0.7 copy.40
  107.1 0.4 reshape.93
  107.5 6.4 %convolution_bitcast_fusion = f32[4,32,32,32]{3,2,1,0:T(8,128)S(1)} fusion(f32[32,32,512,1]{2,1,0,3:T(8,128)} %bitcast.51, f32[4,32,512,1]{2,1,0,3:T(8,128)S(1)} %reshape.93), kind=kOutput, calls=%fused_computation.9 | convolution fusion | flops 805306368 | bytes 2883584 | tf_op jit(solution)/shard_map/dot_general | solution.py:57
  113.9 1.0 reshape.83
  114.9 172.0 %all-to-all-done = f32[32,16,4,1024]{3,2,1,0:T(4,128)} async-done(((f32[32,16,4,1024]{3,2,1,0:T(4,128)}), f32[32,16,4,1024]{3,2,1,0:T(4,128)}, u32[]{:S(2)}, u32[]{:S(2)}) %all-to-all-start) | async-done | bytes 8388640 | tf_op jit(solution)/shard_map/all_to_all | solution.py:28
  286.9 9.2 %while.10 = (s32[]{:T(128)}, f32[128,1024]{1,0:T(8,128)S(1)}, s32[]{:T(128)}, f32[32,16,4,1024]{3,2,1,0:T(4,128)}, f32[16,1024,1024]{2,1,0:T(8,128)}, /*index=5*/s32[]{:T(128)}, s32[]{:T(128)}, s32[]{:T(128)}) while((s32[]{:T(128)}, f32[128,1024]{1,0:T(8,128)S(1)}, s32[]{:T(128)}, f32[32,16,4,1024]{3,2,1,0:T(4,128)}, ...), condition=%wide.region_2.3_spmd, body=%wide.region_1.2_spmd.sunk | while | flops 1610743808 | bytes 7864447 | solution.py:47
  287.5 1.1 constant_dynamic-slice_fusion.4
  288.6 0.2 reshape.99
  288.8 6.7 %fusion.17 = f32[128,1024]{1,0:T(8,128)S(1)} fusion(f32[128,1024]{1,0:T(8,128)S(1)} %get-tuple-element.89, f32[128,1024]{1,0:T(8,128)S(1)} %reshape.99, f32[16,1024,1024]{2,1,0:T(8,128)} %get-tuple-element.100, s32[]{:T(128)S(6)} %select_n.25), kind=kOutput, calls=%fused_computation.4.clone.1 | convolution fusion | flops 1610743808 | bytes 5767172 | tf_op jit(solution)/shard_map/while/body/dot_general | solution.py:38
  296.2 0.8 add.53
  297.0 0.0 all-reduce.3.cloned.1.call-update
  297.0 255.5 %all-reduce.3.cloned.1.call-done = f32[128,1024]{1,0:T(8,128)} async-done(((f32[128,1024]{1,0:T(8,128)}), f32[128,1024]{1,0:T(8,128)}) %all-reduce.3.cloned.1.call-update) | async-done | bytes 524304
  552.5 1.4 constant_dynamic-slice_fusion.1
  (4 shorter events, 0.1 us)
Async XLA Ops:
  9.3 85.7 %all-to-all-start.1 = ((f32[32,1,2048]{2,1,0:T(1,128)}), f32[32,1,2048]{2,1,0:T(1,128)S(1)}, u32[]{:S(2)}, u32[]{:S(2)}) async-start(f32[32,1,2048]{2,1,0:T(1,128)} %reshape.96), calls=%async_computation.1 | async-start | bytes 524288 | tf_op jit(solution)/shard_map/all_to_all | solution.py:49
  16.6 11.1 %copy-start.1 = (s32[32,16,2]{0,2,1:T(2,128)S(1)}, s32[32,16,2]{0,2,1:T(2,128)}, u32[]{:S(2)}) copy-start(s32[32,16,2]{0,2,1:T(2,128)} %param.9) | copy-start | bytes 12292
  95.0 6.2 %copy-start = (f32[16,32,1024]{2,1,0:T(8,128)S(1)}, f32[16,32,1024]{2,1,0:T(8,128)}, u32[]{:S(2)}) copy-start(f32[16,32,1024]{2,1,0:T(8,128)} %param.8) | copy-start | bytes 6291460
  95.0 191.9 %all-to-all-start = ((f32[32,16,4,1024]{3,2,1,0:T(4,128)}), f32[32,16,4,1024]{3,2,1,0:T(4,128)}, u32[]{:S(2)}, u32[]{:S(2)}) async-start(f32[32,16,4,1024]{3,2,1,0:T(4,128)} %broadcast_select_fusion), calls=%async_computation | async-start | bytes 16777216 | tf_op jit(solution)/shard_map/all_to_all | solution.py:28
  100.9 451.6 %all-reduce.3.cloned.1.call-start = ((), (), s32[]{:S(2)}) async-start(), calls=%async_computation.2 | async-start | bytes 1048576
Sparse Core Ops, SparseCore 0:
  297.1 255.3 all-reduce.2
where the time goes:
time: 561 us
  waiting for transfers between devices  427 us (76%)
  local copies, waits for them, and re-layouts  81.5 us (15%)
  between operations  13.5 us (2%)
  starting transfers between devices  13.3 us (2%)
  matrix products  13.1 us (2%)
  other arithmetic  10.5 us (2%)
    unnamed x2, waiting for transfers between devices  256 us
    all_to_all x1, waiting for transfers between devices, body(): lax.all_to_all(outgoing, ('row', 'col'), split_axis=0, concat_axis=0, til...  172 us
    reshape x2, local copies, waits for them, and re-layouts, tile_stack(): shaped = amplitudes.reshape(local_rows, NVT, TB, NVT, TB)  26.9 us
    gather x1, local copies, waits for them, and re-layouts, body(): jnp.take(stacked, pair_ids, axis=0)  22.9 us
    reshape x2, local copies, waits for them, and re-layouts, tile_stack(): jnp.transpose(shaped, (1, 3, 0, 2, 4))  20.5 us
  transfers between devices with their start and end apart: 3, of which 2 were waited for; matrix products, arithmetic and copies ran while one was open for 16% of the time, Pallas kernels for 0%

commit v1 on v0

v1 whole, which is shorter than its diff:
```python
import functools

import jax
import jax.numpy as jnp
from jax import lax
from jax.experimental import pallas as pl
from jax.experimental.pallas import tpu as pltpu
from jax.sharding import PartitionSpec as P

TB = 32
NVT = 16
LANES = 128
GROUP = LANES // TB
SUB = TB * TB // LANES


def pack_kernel(local_rows, slots_all, ids_ref, amp_ref, out_ref, held, sems):
    wide = NVT * TB
    copies = []
    for h in range(wide // LANES):
        for r in range(local_rows):
            n = h * local_rows + r
            copies.append(
                pltpu.make_async_copy(
                    amp_ref.at[r, :, pl.ds(h * LANES, LANES)],
                    held.at[pl.ds(n * wide, wide), :],
                    sems.at[n],
                )
            )
    for copy in copies:
        copy.start()
    for copy in copies:
        copy.wait()
    chunk = lax.broadcasted_iota(jnp.int32, (SUB, LANES), 1) // TB

    def one_slot(k, carry):
        pair = ids_ref[k]

        @pl.when(pair >= 0)
        def _():
            upper = pair // NVT
            lower = pair % NVT
            h = lower // GROUP
            low = lower % GROUP
            for r in range(local_rows):
                base = (h * local_rows + r) * wide + upper * TB
                value = jnp.zeros((SUB, LANES), jnp.float32)
                for j in range(GROUP):
                    x = held[pl.ds(base + j, SUB, stride=GROUP), :]
                    x = pltpu.roll(x, ((j - low + GROUP) % GROUP) * TB, 1)
                    value = jnp.where(chunk == j, x, value)
                out_ref[k, pl.ds(r * SUB, SUB), :] = value

        return carry

    lax.fori_loop(0, slots_all, one_slot, 0)


def pack(amplitudes, ids, slots_all):
    local_rows = amplitudes.shape[0]
    groups = NVT * TB // LANES
    return pl.pallas_call(
        functools.partial(pack_kernel, local_rows, slots_all),
        out_shape=jax.ShapeDtypeStruct((slots_all, local_rows * SUB, LANES), jnp.float32),
        in_specs=[
            pl.BlockSpec(memory_space=pltpu.SMEM),
            pl.BlockSpec(memory_space=pl.ANY),
        ],
        out_specs=pl.BlockSpec(memory_space=pltpu.VMEM),
        scratch_shapes=[
            pltpu.VMEM((groups * local_rows * NVT * TB, LANES), jnp.float32),
            pltpu.SemaphoreType.DMA((groups * local_rows,)),
        ],
        compiler_params=pltpu.CompilerParams(vmem_limit_bytes=32 * 1024 * 1024),
        name="pack",
    )(ids, amplitudes)


def ladder_kernel(rows, count_ref, a_ref, v_ref, out_ref, flat, both, total):
    s = pl.program_id(0)

    @pl.when(s == 0)
    def _():
        total[...] = jnp.zeros_like(total)

    @pl.when(s < count_ref[0])
    def _():
        flat[...] = a_ref[:, 0].reshape(rows * SUB, LANES)
        for k in range(SUB):
            a = flat[pl.ds(k, rows, stride=SUB), :]
            high = a.astype(jnp.bfloat16)
            low = (a - high.astype(jnp.float32)).astype(jnp.bfloat16)
            both[pl.ds(0, rows), pl.ds(k * LANES, LANES)] = high
            both[pl.ds(rows, rows), pl.ds(k * LANES, LANES)] = low
        dims = (((1,), (1,)), ((), ()))
        step = 256
        for i in range(TB * TB // step):
            part = pl.ds(i * step, step)
            v = v_ref[0, part, :]
            vh = v.astype(jnp.bfloat16)
            vl = (v - vh.astype(jnp.float32)).astype(jnp.bfloat16)
            b = both[...]
            total[part, :] += lax.dot_general(
                vh, b, dims, preferred_element_type=jnp.float32
            ) + lax.dot_general(vl, b, dims, preferred_element_type=jnp.float32)

    @pl.when(s == pl.num_programs(0) - 1)
    def _():
        out_ref[...] = (total[:, :rows] + total[:, rows:]).T


def ladder_of(arrived, integrals, count):
    devices_all, slot_total, depth, _ = arrived.shape
    rows = devices_all * depth // SUB
    size = TB * TB

    def at(s, count_ref):
        return jnp.minimum(s, jnp.maximum(count_ref[0] - 1, 0))

    return pl.pallas_call(
        functools.partial(ladder_kernel, rows),
        out_shape=jax.ShapeDtypeStruct((rows, size), jnp.float32),
        grid_spec=pltpu.PrefetchScalarGridSpec(
            num_scalar_prefetch=1,
            grid=(slot_total,),
            in_specs=[
                pl.BlockSpec((devices_all, 1, depth, LANES), lambda s, c: (0, at(s, c), 0, 0)),
                pl.BlockSpec((1, size, size), lambda s, c: (at(s, c), 0, 0)),
            ],
            out_specs=pl.BlockSpec((rows, size), lambda s, c: (0, 0)),
            scratch_shapes=[
                pltpu.VMEM((rows * SUB, LANES), jnp.float32),
                pltpu.VMEM((2 * rows, size), jnp.bfloat16),
                pltpu.VMEM((size, 2 * rows), jnp.float32),
            ],
        ),
        compiler_params=pltpu.CompilerParams(
            dimension_semantics=("arbitrary",), vmem_limit_bytes=32 * 1024 * 1024
        ),
        name="ladder",
    )(count, arrived, integrals)


def body(amplitudes, integrals, coupling, task_table):
    devices_all = lax.axis_size("row") * lax.axis_size("col")
    local_rows = amplitudes.shape[0]
    slot_total = integrals.shape[0]
    total_rows = devices_all * local_rows
    upper, lower = task_table[:, :, 0], task_table[:, :, 1]
    ids = jnp.where(upper >= 0, upper * NVT + lower, -1)

    first_tile = amplitudes[:, :TB, :]
    pieces = lax.all_to_all(first_tile, ("row", "col"), split_axis=2, concat_axis=0, tiled=True)
    outgoing = pack(amplitudes, ids.reshape(-1), devices_all * slot_total).reshape(
        devices_all, slot_total * local_rows * SUB, LANES
    )
    arrived = lax.all_to_all(outgoing, ("row", "col"), split_axis=0, concat_axis=0, tiled=True)
    arrived = arrived.reshape(devices_all, slot_total, local_rows * SUB, LANES)

    own_index = lax.axis_index(("row", "col"))
    own_ids = lax.dynamic_index_in_dim(ids, own_index, 0, keepdims=False)
    count = jnp.sum((own_ids >= 0).astype(jnp.int32)).reshape(1)
    ladder = ladder_of(arrived, integrals, count)

    width_part = pieces.shape[2]
    occupied = coupling.shape[1]
    window = total_rows // occupied
    regrouped = jnp.transpose(
        pieces.reshape(window, occupied, TB, width_part), (0, 2, 3, 1)
    ).reshape(window * TB, width_part * occupied)
    coupling_rows = coupling.reshape(width_part * occupied, occupied * TB)
    hole_term = jnp.dot(
        regrouped,
        coupling_rows,
        precision=lax.Precision.HIGHEST,
        preferred_element_type=jnp.float32,
    )
    hole_term = jnp.transpose(hole_term.reshape(window, TB, occupied, TB), (0, 2, 1, 3)).reshape(
        total_rows, TB * TB
    )
    partial = (ladder + hole_term).reshape(devices_all, local_rows * SUB, LANES)
    shares = lax.all_to_all(partial, ("row", "col"), split_axis=0, concat_axis=0, tiled=True)
    return jnp.sum(shares, axis=0).reshape(local_rows, TB * TB)


def solution(mesh):
    in_specs = (
        P(("row", "col"), None, None),
        P(("row", "col"), None, None),
        P(("row", "col"), None, None),
        P(),
    )
    out_specs = P(("row", "col"), None)
    return jax.shard_map(body, mesh=mesh, in_specs=in_specs, out_specs=out_specs, check_vma=False)
```

time: 561 us -> 285 us (0.51)
  waiting for transfers between devices: 427 us -> 172 us
  local copies, waits for them, and re-layouts: 81.5 us -> 14.2 us
  blocking collectives: 0 us -> 45.4 us
  Pallas kernels: 0 us -> 30.2 us
  between operations: 13.5 us -> 0.15 us
  other arithmetic: 10.5 us -> 2.06 us
  matrix products: 13.1 us -> 6.4 us
    unnamed x2 -> x0, waiting for transfers between devices: 256 us -> none
    reshape x5 -> x2, local copies, waits for them, and re-layouts: 47.6 us -> 0.7 us  [the longest x1 0.62 us: body(): return jnp.sum(shares, axis=0).reshape(local_rows, TB * TB)]
    all_to_all x0 -> x1, blocking collectives: none -> 45.4 us  [body(): lax.all_to_all(partial, ('row', 'col'), split_axis=0, concat_axis=0, tile...]
    pallas_call x0 -> x2, Pallas kernels: none -> 30.2 us  [the longest x1 26.1 us: pack(): pl.pallas_call(functools.partial(pack_kernel, local_rows, slots_all), out...]
    gather x1 -> x0, local copies, waits for them, and re-layouts: 22.9 us -> none  [body(): jnp.take(stacked, pair_ids, axis=0)]
    select_n x1, other arithmetic: 7.73 us -> 0.02 us  [body(): ids = jnp.where(upper >= 0, upper * NVT + lower, -1)]
    dot_general x1 -> x0, matrix products: 6.69 us -> none  [add_tile(): lax.dot_general(tile_rows, integral_tile, (((1,), (1,)), ((), ())), preci...]
  transfers between devices with their start and end apart: 3 -> 2, of which waited for: 2 -> 1; matrix products, arithmetic and copies ran while one was open for 16% -> 5% of each run, Pallas kernels for 0% -> 9%
where the time goes in v1:
time: 285 us; the launch traced here: 284 us
  waiting for transfers between devices  172 us (60%)
  blocking collectives  45.4 us (16%)
  Pallas kernels  30.2 us (11%)
  local copies, waits for them, and re-layouts  14.2 us (5%)
  starting transfers between devices  13.3 us (5%)
  matrix products  6.4 us (2%)
    all_to_all x1, waiting for transfers between devices, body(): lax.all_to_all(outgoing, ('row', 'col'), split_axis=0, concat_axis=0, til...  172 us
    all_to_all x1, blocking collectives, body(): lax.all_to_all(partial, ('row', 'col'), split_axis=0, concat_axis=0, tile...  45.4 us
    pallas_call x1, Pallas kernels, pack(): pl.pallas_call(functools.partial(pack_kernel, local_rows, slots_all), out...  26.1 us
    all_to_all x1, starting transfers between devices, body(): lax.all_to_all(first_tile, ('row', 'col'), split_axis=2, concat_axis=0, t...  7.33 us
    unnamed x10, local copies, waits for them, and re-layouts  7.32 us
    dot_general x1, matrix products, body(): jnp.dot(regrouped, coupling_rows, precision=lax.Precision.HIGHEST, prefer...  6.4 us
    all_to_all x1, starting transfers between devices, body(): lax.all_to_all(outgoing, ('row', 'col'), split_axis=0, concat_axis=0, til...  5.96 us
  transfers between devices with their start and end apart: 2, of which 1 were waited for; matrix products, arithmetic and copies ran while one was open for 5% of the time, Pallas kernels for 9%

profile of v1, /device:TPU:0, one launch (start us, length us, event | category | flops | bytes accessed | tf_op | source)
XLA Modules:
  0.0 284.0 jit_solution(4547583531414929704)
XLA Ops:
  0.0 0.0 copy-start.3
  0.0 1.0 slice.11
  1.0 0.4 copy.12
  1.4 1.4 reshape.65
  2.8 7.3 %all-to-all-start.1 = ((f32[32,1,2048]{2,1,0:T(1,128)}), f32[32,1,2048]{2,1,0:T(1,128)S(1)}, u32[]{:S(2)}, u32[]{:S(2)}) async-start(f32[32,1,2048]{2,1,0:T(1,128)} %reshape.65), calls=%async_computation.1 | async-start | bytes 524288 | tf_op jit(solution)/shard_map/all_to_all | solution.py:153
  10.1 0.0 copy-done.3
  10.1 0.1 copy.11
  10.2 0.1 select_n.15.ids_ref
  10.3 0.0 copy-start.1
  10.3 2.2 copy-done.1
  12.5 26.1 %pack.1 = f32[512,32,128]{2,1,0:T(8,128)S(1)} custom-call(s32[512]{0:T(512)S(1)} %select_n.15.ids_ref, f32[4,512,512]{2,1,0:T(8,128)S(1)} %copy-done.1), custom_call_target="tpu_custom_call" | custom-call | tf_op jit(solution)/shard_map/pack/pallas_call | solution.py:62
  38.5 0.0 copy-start
  38.5 3.2 %copy-done = f32[512,32,128]{2,1,0:T(8,128)} copy-done((f32[512,32,128]{2,1,0:T(8,128)}, f32[512,32,128]{2,1,0:T(8,128)S(1)}, u32[]{:S(2)}) %copy-start) | copy-done | bytes 8388632
  41.8 0.0 all-to-all-done.1
  41.8 0.0 copy-start.2
  41.8 6.0 %all-to-all-start = ((f32[32,512,128]{2,1,0:T(8,128)}), f32[32,512,128]{2,1,0:T(8,128)}, u32[]{:S(2)}, u32[]{:S(2)}) async-start(f32[32,512,128]{2,1,0:T(8,128)} %bitcast.29), calls=%async_computation | async-start | bytes 16777216 | tf_op jit(solution)/shard_map/all_to_all | solution.py:157
  47.7 0.0 copy-done.2
  47.7 1.9 copy.16
  49.6 0.7 fusion.1
  50.3 0.5 broadcast.24
  50.9 1.2 reduce.2
  52.1 0.5 reshape.66
  52.7 0.1 copy.13
  52.7 0.1 copy.14
  52.9 0.7 copy.15
  53.6 0.4 reshape.62
  54.0 6.4 %convolution_bitcast_fusion = f32[4,32,32,32]{3,2,1,0:T(8,128)S(1)} fusion(f32[32,32,512,1]{2,1,0,3:T(8,128)} %bitcast.30, f32[4,32,512,1]{2,1,0,3:T(8,128)S(1)} %reshape.62), kind=kOutput, calls=%fused_computation | convolution fusion | flops 805306368 | bytes 2883584 | tf_op jit(solution)/shard_map/dot_general | solution.py:172
  60.4 1.0 reshape.58
  61.4 172.3 %all-to-all-done = f32[32,512,128]{2,1,0:T(8,128)} async-done(((f32[32,512,128]{2,1,0:T(8,128)}), f32[32,512,128]{2,1,0:T(8,128)}, u32[]{:S(2)}, u32[]{:S(2)}) %all-to-all-start) | async-done | bytes 8388640 | tf_op jit(solution)/shard_map/all_to_all | solution.py:157
  233.6 4.2 %ladder.1 = f32[128,1024]{1,0:T(8,128)S(1)} custom-call(s32[1]{0:T(128)} %bitcast.count_ref, f32[32,16,32,128]{3,2,1,0:T(8,128)} %bitcast.2.a_ref, f32[16,1024,1024]{2,1,0:T(8,128)} %v_ref.1), custom_call_target="tpu_custom_call" | custom-call | tf_op jit(solution)/shard_map/ladder/pallas_call | solution.py:120
  237.8 0.1 add.19
  237.9 0.1 reshape.59
  238.0 45.4 %all_to_all.25 = f32[32,32,128]{2,1,0:T(8,128)S(1)} all-to-all(f32[32,32,128]{2,1,0:T(8,128)S(1)} %reshape.59), channel_id=1, replica_groups=mesh['row'=8,'col'=4] {'row','col'}, dimensions={0} | all-to-all | bytes 1048576 | tf_op jit(solution)/shard_map/all_to_all | solution.py:182
  283.4 0.6 reshape.60
  (2 shorter events, 0.1 us)
Async XLA Ops:
  0.0 10.1 %copy-start.3 = (s32[32,16,2]{0,2,1:T(2,128)S(1)}, s32[32,16,2]{0,2,1:T(2,128)}, u32[]{:S(2)}) copy-start(s32[32,16,2]{0,2,1:T(2,128)} %param.7) | copy-start | bytes 12292
  2.8 39.0 %all-to-all-start.1 = ((f32[32,1,2048]{2,1,0:T(1,128)}), f32[32,1,2048]{2,1,0:T(1,128)S(1)}, u32[]{:S(2)}, u32[]{:S(2)}) async-start(f32[32,1,2048]{2,1,0:T(1,128)} %reshape.65), calls=%async_computation.1 | async-start | bytes 524288 | tf_op jit(solution)/shard_map/all_to_all | solution.py:153
  10.3 2.2 copy-start.1
  38.5 3.2 %copy-start = (f32[512,32,128]{2,1,0:T(8,128)}, f32[512,32,128]{2,1,0:T(8,128)S(1)}, u32[]{:S(2)}) copy-start(f32[512,32,128]{2,1,0:T(8,128)S(1)} %pack.1) | copy-start | bytes 25165828
  41.8 6.0 %copy-start.2 = (f32[16,32,1024]{2,1,0:T(8,128)S(1)}, f32[16,32,1024]{2,1,0:T(8,128)}, u32[]{:S(2)}) copy-start(f32[16,32,1024]{2,1,0:T(8,128)} %param.6) | copy-start | bytes 6291460
  41.8 191.9 %all-to-all-start = ((f32[32,512,128]{2,1,0:T(8,128)}), f32[32,512,128]{2,1,0:T(8,128)}, u32[]{:S(2)}, u32[]{:S(2)}) async-start(f32[32,512,128]{2,1,0:T(8,128)} %bitcast.29), calls=%async_computation | async-start | bytes 16777216 | tf_op jit(solution)/shard_map/all_to_all | solution.py:157
